TPU v7x, 32 devices: a whole 2x2x4 slice. The times are simulated.
32 devices in a mesh: row: 4 (over y, x), col: 8 (over z, core).
Axes of the slice: x: 2, y: 2, z: 4, core: 2. Of those that a mesh axis runs over, the one named last changes fastest.
Arguments:
- user_feats: bfloat16 [4096, 128], P(('row', 'col')), may hold values from -6 to 6
- item_feats: bfloat16 [16384, 128], P(('col', 'row')), may hold values from -6 to 6
- tile_values: bfloat16 [4, 8, 1, 512, 512], P('row', 'col'), may hold values from -0.15625 to 0.15625
- tile_coords: int32 [4, 8, 2, 1], P('row', 'col'), may hold values from 0 to 3, as said below
- tile_count: int32 [4, 8], P('row', 'col'), may hold values from 1 to 1, as said below
Outputs:
- users_next: bfloat16 [4096, 128], P(('row', 'col'))
- items_next: bfloat16 [16384, 128], P(('col', 'row'))
Inputs may be any that keep to these rules, and one draw needn't show every extreme that they name: `tile_coords`: within one device's first tile_count slots the pairs (user tile, item tile) are distinct; the first entry is a user tile below 2, the second an item tile below 4; slots at or after the count carry no tile. `tile_count`: at least one device has all 1 slots live.
All inputs are finite; a program needn't handle non-finite values.
Results may differ from a plain program's by a relative error of at most 0.001.
Values may be sent and summed in bfloat16 or wider, within the bound.
A program may use at most 64 MiB of HBM per device.

v0:
```python
import jax
import jax.numpy as jnp
from jax import lax
from jax.sharding import PartitionSpec as P


def local(user_feats, item_feats, tile_values, tile_coords, tile_count):
    user_block = lax.all_gather(user_feats, "col", axis=0, tiled=True)
    item_block = lax.all_gather(item_feats, "row", axis=0, tiled=True)
    tiles = tile_values[0, 0]
    coords = tile_coords[0, 0]
    count = tile_count[0, 0]
    slots = tiles.shape[0]
    size = tiles.shape[1]
    width = user_block.shape[1]
    user_tiles = user_block.shape[0] // size
    item_tiles = item_block.shape[0] // size
    live = jnp.arange(slots) < count
    pick_user = ((coords[0][:, None] == jnp.arange(user_tiles)[None, :]) & live[:, None]).astype(
        jnp.bfloat16
    )
    pick_item = (coords[1][:, None] == jnp.arange(item_tiles)[None, :]).astype(jnp.bfloat16)
    user_sel = jnp.einsum(
        "su,uiw->siw",
        pick_user,
        user_block.reshape(user_tiles, size, width),
        preferred_element_type=jnp.float32,
    ).astype(jnp.bfloat16)
    item_sel = jnp.einsum(
        "st,tjw->sjw",
        pick_item,
        item_block.reshape(item_tiles, size, width),
        preferred_element_type=jnp.float32,
    ).astype(jnp.bfloat16)
    to_users = jnp.einsum("sij,sjw->siw", tiles, item_sel, preferred_element_type=jnp.float32)
    to_items = jnp.einsum("sij,siw->sjw", tiles, user_sel, preferred_element_type=jnp.float32)
    part_users = jnp.einsum(
        "su,siw->uiw", pick_user.astype(jnp.float32), to_users, precision=lax.Precision.HIGHEST
    ).reshape(user_tiles * size, width)
    part_items = jnp.einsum(
        "st,sjw->tjw", pick_item.astype(jnp.float32), to_items, precision=lax.Precision.HIGHEST
    ).reshape(item_tiles * size, width)
    users_next = lax.psum_scatter(part_users, "col", scatter_dimension=0, tiled=True)
    items_next = lax.psum_scatter(part_items, "row", scatter_dimension=0, tiled=True)
    return (users_next.astype(jnp.bfloat16), items_next.astype(jnp.bfloat16))


def solution(mesh):
    placed = (
        P(("row", "col"), None),
        P(("col", "row"), None),
        P("row", "col", None, None, None),
        P("row", "col", None, None),
        P("row", "col"),
    )
    return jax.shard_map(
        local,
        mesh=mesh,
        in_specs=placed,
        out_specs=(P(("row", "col"), None), P(("col", "row"), None)),
        check_vma=False,
    )
```

profile of v0, /device:TPU:0, one launch (start us, length us, event | category | flops | bytes accessed | tf_op | source)
XLA Modules:
  0.0 93.8 jit_solution(1561451656250529168)
XLA Ops:
  7.2 0.0 copy-start
  7.2 0.0 reduce-scatter.3.cloned.1.call-start
  7.2 1.3 %fusion.14 = (s32[1,1,1,1]{2,3,1,0:T(1,128)}, s32[1,1,1,1]{2,3,1,0:T(1,128)}) fusion(s32[1,1,2,1]{2,3,1,0:T(1,128)} %param.8), kind=kLoop, calls=%fused_computation.22 | loop fusion | bytes 16 | tf_op jit(solution)/shard_map/slice | solution.py:19
  9.2 11.9 %all_gather.6 = bf16[2048,128]{1,0:T(8,128)(2,1)S(1)} all-gather(bf16[512,128]{1,0:T(8,128)(2,1)} %param.6), channel_id=1, replica_groups=mesh['row'=4,'col'=8] {'row'}, dimensions={0}, use_global_device_ids=true | all-gather | bytes 655360 | tf_op jit(solution)/shard_map/all_gather | solution.py:9
  21.1 1.1 %fusion.2 = f32[1,512,128]{2,0,1:T(1,128)S(1)} fusion(bf16[4,512,128]{2,1,0:T(8,128)(2,1)S(1)} %bitcast.32, s32[]{:T(128)} %bitcast.2), kind=kOutput, calls=%fused_computation.5 | convolution fusion | flops 524292 | bytes 786436 | tf_op jit(solution)/shard_map/st,tjw->sjw/dot_general | solution.py:29
  22.2 0.0 copy-done
  22.2 0.3 convolution_bitcast_fusion.1
  22.5 0.1 copy.7
  22.7 0.7 and_convert_fusion
  23.3 0.9 broadcast_multiply_fusion.1
  24.2 0.0 copy-start.1
  24.2 0.0 reduce-scatter.3.cloned.1.call-update
  24.3 0.0 reduce-scatter.5.cloned.1.call-start
  24.3 0.7 copy-done.1
  25.0 14.4 %all_gather.7 = bf16[1024,128]{1,0:T(8,128)(2,1)S(1)} all-gather(bf16[128,128]{1,0:T(8,128)(2,1)S(1)} %copy-done.1), channel_id=1, replica_groups=mesh['row'=4,'col'=8] {'col'}, dimensions={0}, use_global_device_ids=true | all-gather | bytes 294912 | tf_op jit(solution)/shard_map/all_gather | solution.py:8
  39.4 1.1 %fusion.4 = f32[1,512,128]{2,0,1:T(1,128)S(1)} fusion(bf16[2,512,128]{2,1,0:T(8,128)(2,1)S(1)} %bitcast.33, pred[]{:T(512)} %bitcast.1, s32[]{:T(128)} %bitcast), kind=kOutput, calls=%fused_computation.8 | convolution fusion | flops 262148 | bytes 524293 | tf_op jit(solution)/shard_map/su,uiw->siw/dot_general | solution.py:23
  40.5 0.2 convolution_bitcast_fusion
  40.7 0.1 copy.8
  40.9 0.7 compare_convert_fusion
  41.5 1.1 %broadcast_multiply_fusion = f32[4,512,128]{2,1,0:T(8,128)} fusion(f32[512,128]{1,0:T(8,128)S(1)} %copy.8, f32[4]{0:T(128)S(1)} %compare_convert_fusion), kind=kLoop, calls=%fused_computation.4 | loop fusion | flops 262144 | bytes 1310736 | tf_op jit(solution)/shard_map/st,sjw->tjw/dot_general | solution.py:40
  42.6 0.0 reduce-scatter.5.cloned.1.call-update
  42.7 13.4 %reduce-scatter.3.cloned.1.call-done = f32[128,128]{1,0:T(8,128)} async-done(((f32[1024,128]{1,0:T(8,128)}), f32[128,128]{1,0:T(8,128)}) %reduce-scatter.3.cloned.1.call-update) | async-done | bytes 65552 | tf_op jit(solution)/shard_map/reduce_scatter | solution.py:43
  56.1 1.5 %convert_element_type.19 = bf16[128,128]{1,0:T(8,128)(2,1)} convert(f32[128,128]{1,0:T(8,128)} %reduce-scatter.3.cloned.1.call-done) | non-fusion elementwise | flops 16384 | bytes 98304 | tf_op jit(solution)/shard_map/convert_element_type | solution.py:45
  57.6 27.8 %reduce-scatter.5.cloned.1.call-done = f32[512,128]{1,0:T(8,128)} async-done(((f32[2048,128]{1,0:T(8,128)}), f32[512,128]{1,0:T(8,128)}) %reduce-scatter.5.cloned.1.call-update) | async-done | bytes 262160 | tf_op jit(solution)/shard_map/reduce_scatter | solution.py:44
  85.3 1.6 %convert_element_type.21 = bf16[512,128]{1,0:T(8,128)(2,1)} convert(f32[512,128]{1,0:T(8,128)} %reduce-scatter.5.cloned.1.call-done) | non-fusion elementwise | flops 65536 | bytes 393216 | tf_op jit(solution)/shard_map/convert_element_type | solution.py:45
Async XLA Ops:
  7.2 15.0 %copy-start = (bf16[1,1,1,512,512]{4,3,2,1,0:T(8,128)(2,1)S(1)}, bf16[1,1,1,512,512]{4,3,2,1,0:T(8,128)(2,1)}, u32[]{:S(2)}) copy-start(bf16[1,1,1,512,512]{4,3,2,1,0:T(8,128)(2,1)} %param.7) | copy-start | bytes 1572868
  7.2 48.9 %reduce-scatter.3.cloned.1.call-start = ((), (), s32[]{:S(2)}) async-start(), calls=%async_computation.2 | async-start | bytes 589824 | tf_op jit(solution)/shard_map/reduce_scatter | solution.py:43
  24.2 0.8 copy-start.1
  24.3 61.1 %reduce-scatter.5.cloned.1.call-start = ((), (), s32[]{:S(2)}) async-start(), calls=%async_computation.3 | async-start | bytes 1310720 | tf_op jit(solution)/shard_map/reduce_scatter | solution.py:44
Sparse Core Ops, SparseCore 0:
  24.4 31.6 reduce-scatter.2
  59.0 26.2 reduce-scatter.4
where the time goes:
time: 94.2 us; the launch traced here: 93.8 us
  waiting for transfers between devices  41.2 us (44%)
  blocking collectives  26.3 us (28%)
  between operations  14.8 us (16%)
  other arithmetic  6.4 us (7%)
  matrix products  2.75 us (3%)
  local copies, waits for them, and re-layouts  2.26 us (2%)
    reduce_scatter x1, waiting for transfers between devices, local(): lax.psum_scatter(part_items, 'row', scatter_dimension=0, tiled=True)  27.8 us
    all_gather x1, blocking collectives, local(): user_block = lax.all_gather(user_feats, 'col', axis=0, tiled=True)  14.4 us
    reduce_scatter x1, waiting for transfers between devices, local(): lax.psum_scatter(part_users, 'col', scatter_dimension=0, tiled=True)  13.4 us
    all_gather x1, blocking collectives, local(): item_block = lax.all_gather(item_feats, 'row', axis=0, tiled=True)  11.9 us
    convert_element_type x2, other arithmetic, local(): return (users_next.astype(jnp.bfloat16), items_next.astype(jnp.bfloat16))  3.08 us
  transfers between devices with their start and end apart: 2, of which 2 were waited for; matrix products, arithmetic and copies ran while one was open for 5% of the time, Pallas kernels for 0%

commit v1 on v0

--- a/solution.py
+++ b/solution.py
@@ -1,10 +1,16 @@
+import functools
+
 import jax
 import jax.numpy as jnp
 from jax import lax
+from jax.experimental import pallas as pl
+from jax.experimental.pallas import tpu as pltpu
 from jax.sharding import PartitionSpec as P
 
-
-def local(user_feats, item_feats, tile_values, tile_coords, tile_count):
+MESH = pl.DeviceIdType.MESH
+
+
+def gathered(user_feats, item_feats, tile_values, tile_coords, tile_count):
     user_block = lax.all_gather(user_feats, "col", axis=0, tiled=True)
     item_block = lax.all_gather(item_feats, "row", axis=0, tiled=True)
     tiles = tile_values[0, 0]
@@ -45,7 +51,271 @@
     return (users_next.astype(jnp.bfloat16), items_next.astype(jnp.bfloat16))
 
 
+def kernel(
+    n_z,
+    coords,
+    count,
+    user_in,
+    item_in,
+    tile_in,
+    out_u,
+    out_i,
+    u_all,
+    i_all,
+    tile_v,
+    tile_t,
+    meta,
+    meta_x,
+    meta_y,
+    meta_p,
+    part_u,
+    from_p,
+    send_z,
+    from_z,
+    part_i,
+    from_1,
+    send_2,
+    from_2,
+    load_sem,
+    meta_s,
+    meta_r,
+    uz_s,
+    uz_r,
+    up_s,
+    up_r,
+    ig_s,
+    ig_r,
+    rp_s,
+    rp_r,
+    rz_s,
+    rz_r,
+    r1_s,
+    r1_r,
+    r2_s,
+    r2_r,
+):
+    row, col = lax.axis_index("row"), lax.axis_index("col")
+    y, x = row // 2, row % 2
+    z, core = col // 2, col % 2
+    row_x, row_y = 2 * y + 1 - x, 2 * (1 - y) + x
+    x_dev, y_dev = (row_x, col), (row_y, col)
+    p_dev = (row, 2 * z + 1 - core)
+    z_devs = [(row, 2 * ((z + d) % n_z) + core) for d in range(n_z)]
+    rows_u, rows_i = user_in.shape[0], item_in.shape[0]
+    size = tile_v.shape[0]
+    half, chunk = rows_i // 2, rows_i // 4
+    pieces = size // rows_u // 2
+
+    def user_slot(at):
+        blocks = size // rows_u
+        inner = pl.multiple_of(at % blocks * rows_u, rows_u)
+        return u_all.at[at // blocks, pl.ds(inner, rows_u)]
+
+    def item_slot(at, part):
+        return i_all.at[at, pl.ds(part * half, half)]
+
+    def copy(src, dst, sends, recvs, at, device):
+        return pltpu.make_async_remote_copy(
+            src_ref=src,
+            dst_ref=dst,
+            send_sem=sends.at[at],
+            recv_sem=recvs.at[at],
+            device_id=device,
+            device_id_type=MESH,
+        )
+
+    loads = [
+        pltpu.make_async_copy(user_in, user_slot(col), load_sem.at[0]),
+        pltpu.make_async_copy(item_in, i_all.at[row], load_sem.at[1]),
+        pltpu.make_async_copy(tile_in, tile_v, load_sem.at[2]),
+    ]
+    for load in loads:
+        load.start()
+
+    barrier = pltpu.get_barrier_semaphore()
+    peers = [x_dev, y_dev, p_dev] + z_devs[1:]
+    for peer in peers:
+        pl.semaphore_signal(barrier, inc=1, device_id=peer, device_id_type=MESH)
+    tu, ti = coords[0], coords[1]
+    meta[0] = jnp.full(meta.shape[1:], tu, jnp.int32)
+    meta[1] = jnp.full(meta.shape[1:], ti, jnp.int32)
+    meta[2] = jnp.full(meta.shape[1:], count[0], jnp.int32)
+    my_tu, my_ti, live = meta[0][0:1, :], meta[1][0:1, :], meta[2][0:1, :] > 0
+    pl.semaphore_wait(barrier, len(peers))
+
+    sent = []
+
+    def start(c):
+        c.start()
+        sent.append(c)
+
+    loads[0].wait()
+    for d in range(1, n_z):
+        start(copy(user_slot(col), user_slot(col), uz_s, uz_r, d, z_devs[d]))
+    start(copy(user_slot(col), user_slot(col), up_s, up_r, 0, p_dev))
+    loads[1].wait()
+    start(copy(item_slot(row, 0), item_slot(row, 0), ig_s, ig_r, 0, x_dev))
+    start(copy(item_slot(row, 1), item_slot(row, 1), ig_s, ig_r, 1, y_dev))
+    start(copy(item_slot(row, 1), item_slot(row, 1), ig_s, ig_r, 2, x_dev))
+    start(copy(item_slot(row, 0), item_slot(row, 0), ig_s, ig_r, 3, y_dev))
+    start(copy(meta, meta_x, meta_s, meta_r, 0, x_dev))
+    start(copy(meta, meta_y, meta_s, meta_r, 1, y_dev))
+    start(copy(meta, meta_p, meta_s, meta_r, 2, p_dev))
+
+    loads[2].wait()
+    tile_t[...] = tile_v[...].T
+
+    def arrived(slot, recvs, at):
+        copy(slot, slot, recvs, recvs, at, x_dev).wait_recv()
+
+    arrived(item_slot(row_x, 0), ig_r, 0)
+    start(copy(item_slot(row_x, 0), item_slot(row_x, 0), ig_s, ig_r, 4, y_dev))
+    arrived(item_slot(row_y, 1), ig_r, 1)
+    start(copy(item_slot(row_y, 1), item_slot(row_y, 1), ig_s, ig_r, 5, x_dev))
+    order = [1] + list(range(n_z - 1, 1, -1)) if n_z > 1 else []
+    for d in order:
+        slot = user_slot(2 * ((z - d + n_z) % n_z) + core)
+        arrived(slot, uz_r, d)
+        start(copy(slot, slot, up_s, up_r, d, p_dev))
+    for d in [0] + order:
+        arrived(user_slot(2 * ((z - d + n_z) % n_z) + 1 - core), up_r, d)
+
+    user_sel = u_all[tu]
+    user_sel = jnp.where(live, user_sel, 0.0).astype(user_sel.dtype)
+    part_i[...] = jnp.dot(
+        tile_t[...], user_sel, preferred_element_type=jnp.float32
+    ).reshape(part_i.shape)
+    for c in (0, 2, 1, 3):
+        start(copy(part_i.at[c], from_1.at[c], r1_s, r1_r, c, x_dev if c < 2 else y_dev))
+
+    diagonal = 2 * (1 - y) + 1 - x
+    arrived(item_slot(row_x, 1), ig_r, 2)
+    arrived(item_slot(row_y, 0), ig_r, 3)
+    arrived(item_slot(diagonal, 0), ig_r, 4)
+    arrived(item_slot(diagonal, 1), ig_r, 5)
+    item_sel = i_all[ti]
+    item_sel = jnp.where(live, item_sel, 0.0).astype(item_sel.dtype)
+    part_u[...] = jnp.dot(
+        tile_v[...], item_sel, preferred_element_type=jnp.float32
+    ).reshape(part_u.shape)
+    for h in range(pieces):
+        start(copy(part_u.at[2 * h + 1 - core], from_p.at[h], rp_s, rp_r, h, p_dev))
+
+    arrived(meta_x, meta_r, 0)
+    arrived(meta_y, meta_r, 1)
+    arrived(meta_p, meta_r, 2)
+
+    def second(c):
+        other, owner, device = (
+            (meta_x, row_y, y_dev) if c < 2 else (meta_y, row_x, x_dev)
+        )
+        theirs = other[1][0:1, :]
+        arrived(from_1.at[c], r1_r, c)
+        send_2[c] = jnp.where(my_ti == owner, part_i[c], 0.0) + jnp.where(
+            theirs == owner, from_1[c], 0.0
+        )
+        start(copy(send_2.at[c], from_2.at[c], r2_s, r2_r, c, device))
+
+    second(0)
+    second(2)
+
+    partner_tu = meta_p[0][0:1, :]
+    for h in range(pieces):
+        arrived(from_p.at[h], rp_r, h)
+    for d in list(range(1, n_z)) + [0]:
+        at = (z + d) % n_z
+        tile, h = at // pieces, at % pieces
+        send_z[d] = jnp.where(my_tu == tile, part_u[2 * h + core], 0.0) + jnp.where(
+            partner_tu == tile, from_p[h], 0.0
+        )
+        if d:
+            start(copy(send_z.at[d], from_z.at[d], rz_s, rz_r, d, z_devs[d]))
+
+    second(1)
+    second(3)
+
+    for c in (0, 2, 1, 3):
+        theirs = (meta_x if c < 2 else meta_y)[1][0:1, :]
+        mine = jnp.where(my_ti == row, part_i[c], 0.0) + jnp.where(theirs == row, from_1[c], 0.0)
+        arrived(from_2.at[c], r2_r, c)
+        out_i[pl.ds(c * chunk, chunk), :] = (mine + from_2[c]).astype(out_i.dtype)
+
+    total = send_z[0]
+    for d in order:
+        arrived(from_z.at[d], rz_r, d)
+        total = total + from_z[d]
+    out_u[...] = total.astype(out_u.dtype)
+
+    for c in sent:
+        c.wait_send()
+
+
+def planned(user_feats, item_feats, tile_values, tile_coords, tile_count, *, n_z):
+    rows_u, width = user_feats.shape
+    rows_i = item_feats.shape[0]
+    size = tile_values.shape[-1]
+    f32, bf16, dma = jnp.float32, jnp.bfloat16, pltpu.SemaphoreType.DMA
+    blocks = size // rows_u
+    vmem = pl.BlockSpec(memory_space=pltpu.VMEM)
+    smem = pl.BlockSpec(memory_space=pltpu.SMEM)
+    anywhere = pl.BlockSpec(memory_space=pl.ANY)
+    quarter = (4, rows_i // 4, width)
+    pairs = [3, n_z, n_z, 6, blocks // 2, n_z, 4, 4]
+    return pl.pallas_call(
+        functools.partial(kernel, n_z),
+        out_shape=(
+            jax.ShapeDtypeStruct((rows_u, width), bf16),
+            jax.ShapeDtypeStruct((rows_i, width), bf16),
+        ),
+        in_specs=[smem, smem, anywhere, anywhere, anywhere],
+        out_specs=(vmem, vmem),
+        scratch_shapes=[
+            pltpu.VMEM((2 * n_z * rows_u // size, size, width), bf16),
+            pltpu.VMEM((4, rows_i, width), bf16),
+            pltpu.VMEM((size, size), bf16),
+            pltpu.VMEM((size, size), bf16),
+            pltpu.VMEM((3, 8, width), jnp.int32),
+            pltpu.VMEM((3, 8, width), jnp.int32),
+            pltpu.VMEM((3, 8, width), jnp.int32),
+            pltpu.VMEM((3, 8, width), jnp.int32),
+            pltpu.VMEM((blocks, rows_u, width), f32),
+            pltpu.VMEM((blocks // 2, rows_u, width), f32),
+            pltpu.VMEM((n_z, rows_u, width), f32),
+            pltpu.VMEM((n_z, rows_u, width), f32),
+            pltpu.VMEM(quarter, f32),
+            pltpu.VMEM(quarter, f32),
+            pltpu.VMEM(quarter, f32),
+            pltpu.VMEM(quarter, f32),
+            dma((3,)),
+        ]
+        + [dma((n,)) for n in pairs for _ in range(2)],
+        compiler_params=pltpu.CompilerParams(collective_id=0, has_side_effects=True),
+    )(
+        tile_coords.reshape(2),
+        tile_count.reshape(1),
+        user_feats,
+        item_feats,
+        tile_values.reshape(size, size),
+    )
+
+
 def solution(mesh):
+    n_row, n_col = mesh.shape["row"], mesh.shape["col"]
+
+    def local(user_feats, item_feats, tile_values, tile_coords, tile_count):
+        slots, size = tile_values.shape[2], tile_values.shape[3]
+        rows_u = user_feats.shape[0]
+        fits = (
+            n_row == 4
+            and n_col % 2 == 0
+            and slots == 1
+            and item_feats.shape[0] == size
+            and size % (2 * rows_u) == 0
+            and n_col * rows_u % size == 0
+        )
+        args = (user_feats, item_feats, tile_values, tile_coords, tile_count)
+        return planned(*args, n_z=n_col // 2) if fits else gathered(*args)
+
     placed = (
         P(("row", "col"), None),
         P(("col", "row"), None),

time: 94.2 us -> 27.1 us (0.29)
  waiting for transfers between devices: 41.2 us -> 0 us
  blocking collectives: 26.3 us -> 0 us
  Pallas kernels: 0 us -> 22.7 us
  between operations: 14.8 us -> 1.29 us
  other arithmetic: 6.4 us -> 0 us
  matrix products: 2.75 us -> 0 us
    reduce_scatter x2 -> x0, waiting for transfers between devices: 41.2 us -> none  [the longest x1 27.8 us: local(): lax.psum_scatter(part_items, 'row', scatter_dimension=0, tiled=True)]
    all_gather x2 -> x0, blocking collectives: 26.3 us -> none  [the longest x1 14.4 us: local(): user_block = lax.all_gather(user_feats, 'col', axis=0, tiled=True)]
    pallas_call x0 -> x1, Pallas kernels: none -> 22.7 us  [planned(): pl.pallas_call(functools.partial(kernel, n_z), out_shape=(jax.ShapeDtypeS...]
    convert_element_type x2 -> x0, other arithmetic: 3.08 us -> none  [local(): return (users_next.astype(jnp.bfloat16), items_next.astype(jnp.bfloat16))]
    dot_general x4 -> x0, matrix products: 2.75 us -> none  [the longest x1 1.13 us: local(): jnp.einsum('st,tjw->sjw', pick_item, item_block.reshape(item_tiles, size,...]
    unnamed x4 -> x2, local copies, waits for them, and re-layouts: 0.69 us -> 2.94 us
    dot_general x2 -> x0, other arithmetic: 2.02 us -> none  [the longest x1 1.1 us: local(): jnp.einsum('st,sjw->tjw', pick_item.astype(jnp.float32), to_items, precis...]
    slice x1 -> x0, local copies, waits for them, and re-layouts: 1.31 us -> none  [local(): coords[0][:, None] == jnp.arange(user_tiles)[None, :]]
  transfers between devices with their start and end apart: 2 -> 0, of which waited for: 2 -> 0; matrix products, arithmetic and copies ran while one was open for 5% -> 0% of each run, Pallas kernels for 0% -> 0%
where the time goes in v1:
time: 27.1 us; the launch traced here: 26.9 us
  Pallas kernels  22.7 us (84%)
  local copies, waits for them, and re-layouts  2.94 us (11%)
  between operations  1.29 us (5%)
    pallas_call x1, Pallas kernels, planned(): pl.pallas_call(functools.partial(kernel, n_z), out_shape=(jax.ShapeDtypeS...  22.7 us
    unnamed x2, local copies, waits for them, and re-layouts  2.94 us

profile of v1, /device:TPU:0, one launch (start us, length us, event | category | flops | bytes accessed | tf_op | source)
XLA Modules:
  0.0 26.9 jit_solution(4410485600039606210)
XLA Ops:
  1.3 22.7 %shard_map.68 = (bf16[128,128]{1,0:T(8,128)(2,1)}, bf16[512,128]{1,0:T(8,128)(2,1)}) custom-call(s32[2]{0:T(128)} %bitcast.5, s32[1]{0:T(128)} %bitcast.3.count, bf16[128,128]{1,0:T(8,128)(2,1)} %user_in.1, bf16[512,128]{1,0:T(8,128)(2,1)} %item_in.1, bf16[512,512]{1,0:T(8,128)(2,1)} %bitcast.4), custom_call_target="tpu_custom_call" | custom-call | tf_op jit(solution)/shard_map/pallas_call | solution.py:264
  24.0 1.4 %copy.10 = bf16[128,128]{1,0:T(8,128)(2,1)} copy(bf16[128,128]{1,0:T(8,128)(2,1)} %get-tuple-element.4) | data formatting | bytes 65536
  25.3 1.6 %copy.11 = bf16[512,128]{1,0:T(8,128)(2,1)} copy(bf16[512,128]{1,0:T(8,128)(2,1)} %get-tuple-element.5) | data formatting | bytes 262144

commit v2 on v1

--- a/solution.py
+++ b/solution.py
@@ -139,7 +139,7 @@
     tu, ti = coords[0], coords[1]
     meta[0] = jnp.full(meta.shape[1:], tu, jnp.int32)
     meta[1] = jnp.full(meta.shape[1:], ti, jnp.int32)
-    meta[2] = jnp.full(meta.shape[1:], count[0], jnp.int32)
+    meta[2] = jnp.full(meta.shape[1:], count[0, 0], jnp.int32)
     my_tu, my_ti, live = meta[0][0:1, :], meta[1][0:1, :], meta[2][0:1, :] > 0
     pl.semaphore_wait(barrier, len(peers))
 
@@ -216,9 +216,6 @@
         )
         start(copy(send_2.at[c], from_2.at[c], r2_s, r2_r, c, device))
 
-    second(0)
-    second(2)
-
     partner_tu = meta_p[0][0:1, :]
     for h in range(pieces):
         arrived(from_p.at[h], rp_r, h)
@@ -231,8 +228,8 @@
         if d:
             start(copy(send_z.at[d], from_z.at[d], rz_s, rz_r, d, z_devs[d]))
 
-    second(1)
-    second(3)
+    for c in (0, 2, 1, 3):
+        second(c)
 
     for c in (0, 2, 1, 3):
         theirs = (meta_x if c < 2 else meta_y)[1][0:1, :]
@@ -248,6 +245,17 @@
 
     for c in sent:
         c.wait_send()
+
+
+def put(users, items, out_u, out_i, sems):
+    copies = [
+        pltpu.make_async_copy(users, out_u, sems.at[0]),
+        pltpu.make_async_copy(items, out_i, sems.at[1]),
+    ]
+    for c in copies:
+        c.start()
+    for c in copies:
+        c.wait()
 
 
 def planned(user_feats, item_feats, tile_values, tile_coords, tile_count, *, n_z):
@@ -261,12 +269,9 @@
     anywhere = pl.BlockSpec(memory_space=pl.ANY)
     quarter = (4, rows_i // 4, width)
     pairs = [3, n_z, n_z, 6, blocks // 2, n_z, 4, 4]
-    return pl.pallas_call(
+    outs = pl.pallas_call(
         functools.partial(kernel, n_z),
-        out_shape=(
-            jax.ShapeDtypeStruct((rows_u, width), bf16),
-            jax.ShapeDtypeStruct((rows_i, width), bf16),
-        ),
+        out_shape=(pltpu.VMEM((rows_u, width), bf16), pltpu.VMEM((rows_i, width), bf16)),
         in_specs=[smem, smem, anywhere, anywhere, anywhere],
         out_specs=(vmem, vmem),
         scratch_shapes=[
@@ -292,11 +297,18 @@
         compiler_params=pltpu.CompilerParams(collective_id=0, has_side_effects=True),
     )(
         tile_coords.reshape(2),
-        tile_count.reshape(1),
+        tile_count,
         user_feats,
         item_feats,
         tile_values.reshape(size, size),
     )
+    return pl.pallas_call(
+        put,
+        out_shape=[jax.ShapeDtypeStruct(out.shape, out.dtype) for out in outs],
+        in_specs=[vmem, vmem],
+        out_specs=[anywhere, anywhere],
+        scratch_shapes=[dma((2,))],
+    )(*[pltpu.with_memory_space_constraint(out, pltpu.VMEM) for out in outs])
 
 
 def solution(mesh):

time: 27.1 us -> 23.3 us (0.86)
  local copies, waits for them, and re-layouts: 2.94 us -> 0 us
  Pallas kernels: 22.7 us -> 21.7 us
    unnamed x2 -> x0, local copies, waits for them, and re-layouts: 2.94 us -> none
    pallas_call x1 -> x2, Pallas kernels: 22.7 us -> 21.7 us  [the longest x1 21 us: planned(): pl.pallas_call(functools.partial(kernel, n_z), out_shape=(pltpu.VMEM((row...]
where the time goes in v2:
time: 23.3 us; the launch traced here: 23 us
  Pallas kernels  21.7 us (93%)
  between operations  1.29 us (6%)
    pallas_call x1, Pallas kernels, planned(): pl.pallas_call(functools.partial(kernel, n_z), out_shape=(pltpu.VMEM((row...  21 us
    pallas_call x1, Pallas kernels, planned(): pl.pallas_call(put, out_shape=[jax.ShapeDtypeStruct(out.shape, out.dtype)...  0.69 us

profile of v2, /device:TPU:0, one launch (start us, length us, event | category | flops | bytes accessed | tf_op | source)
XLA Modules:
  0.0 23.0 jit_solution(4229818756918199680)
XLA Ops:
  1.3 21.0 %shard_map.68 = (bf16[128,128]{1,0:T(8,128)(2,1)S(1)}, bf16[512,128]{1,0:T(8,128)(2,1)S(1)}) custom-call(s32[2]{0:T(128)} %bitcast.3, s32[1,1]{1,0:T(1,128)S(6)} %copy.7.count, bf16[128,128]{1,0:T(8,128)(2,1)} %user_in.1, bf16[512,128]{1,0:T(8,128)(2,1)} %item_in.1, bf16[512,512]{1,0:T(8,128)(2,1)} %bitcast.2), custom_call_target="tpu_custom_call" | custom-call | tf_op jit(solution)/shard_map/pallas_call | solution.py:272
  22.3 0.7 %shard_map.69 = (bf16[128,128]{1,0:T(8,128)(2,1)}, bf16[512,128]{1,0:T(8,128)(2,1)}) custom-call(bf16[128,128]{1,0:T(8,128)(2,1)S(1)} %get-tuple-element.4.users, bf16[512,128]{1,0:T(8,128)(2,1)S(1)} %get-tuple-element.5.items), custom_call_target="tpu_custom_call" | custom-call | tf_op jit(solution)/shard_map/pallas_call | solution.py:305

commit v3 on v2

--- a/solution.py
+++ b/solution.py
@@ -53,8 +53,8 @@
 
 def kernel(
     n_z,
-    coords,
-    count,
+    coords_in,
+    count_in,
     user_in,
     item_in,
     tile_in,
@@ -76,6 +76,8 @@
     from_1,
     send_2,
     from_2,
+    coords,
+    count,
     load_sem,
     meta_s,
     meta_r,
@@ -100,7 +102,17 @@
     row_x, row_y = 2 * y + 1 - x, 2 * (1 - y) + x
     x_dev, y_dev = (row_x, col), (row_y, col)
     p_dev = (row, 2 * z + 1 - core)
-    z_devs = [(row, 2 * ((z + d) % n_z) + core) for d in range(n_z)]
+
+    def far_first(at):
+        flip = z // (n_z // 2)
+        mirrored = z + flip * (n_z - 1 - 2 * z)
+        to = n_z - 1 - at
+        to = jnp.where(to <= mirrored, to - 1, to)
+        return to + flip * (n_z - 1 - 2 * to)
+
+    others = [far_first(at) for at in range(n_z - 1)]
+    z_devs = [(row, 2 * at + core) for at in others]
+    near_first = others[::-1]
     rows_u, rows_i = user_in.shape[0], item_in.shape[0]
     size = tile_v.shape[0]
     half, chunk = rows_i // 2, rows_i // 4
@@ -114,28 +126,32 @@
     def item_slot(at, part):
         return i_all.at[at, pl.ds(part * half, half)]
 
-    def copy(src, dst, sends, recvs, at, device):
+    def copy(src, dst, sends, recvs, at, device, to=None):
         return pltpu.make_async_remote_copy(
             src_ref=src,
             dst_ref=dst,
-            send_sem=sends.at[at],
+            send_sem=sends.at[at if to is None else to],
             recv_sem=recvs.at[at],
             device_id=device,
             device_id_type=MESH,
         )
 
+    barrier = pltpu.get_barrier_semaphore()
+    peers = [x_dev, y_dev, p_dev] + z_devs
+    for peer in peers:
+        pl.semaphore_signal(barrier, inc=1, device_id=peer, device_id_type=MESH)
     loads = [
         pltpu.make_async_copy(user_in, user_slot(col), load_sem.at[0]),
         pltpu.make_async_copy(item_in, i_all.at[row], load_sem.at[1]),
         pltpu.make_async_copy(tile_in, tile_v, load_sem.at[2]),
+        pltpu.make_async_copy(coords_in, coords, load_sem.at[3]),
+        pltpu.make_async_copy(count_in, count, load_sem.at[4]),
     ]
     for load in loads:
         load.start()
 
-    barrier = pltpu.get_barrier_semaphore()
-    peers = [x_dev, y_dev, p_dev] + z_devs[1:]
-    for peer in peers:
-        pl.semaphore_signal(barrier, inc=1, device_id=peer, device_id_type=MESH)
+    loads[3].wait()
+    loads[4].wait()
     tu, ti = coords[0], coords[1]
     meta[0] = jnp.full(meta.shape[1:], tu, jnp.int32)
     meta[1] = jnp.full(meta.shape[1:], ti, jnp.int32)
@@ -150,9 +166,9 @@
         sent.append(c)
 
     loads[0].wait()
-    for d in range(1, n_z):
-        start(copy(user_slot(col), user_slot(col), uz_s, uz_r, d, z_devs[d]))
-    start(copy(user_slot(col), user_slot(col), up_s, up_r, 0, p_dev))
+    for to, device in zip(others, z_devs):
+        start(copy(user_slot(col), user_slot(col), uz_s, uz_r, z, device, to))
+    start(copy(user_slot(col), user_slot(col), up_s, up_r, z, p_dev))
     loads[1].wait()
     start(copy(item_slot(row, 0), item_slot(row, 0), ig_s, ig_r, 0, x_dev))
     start(copy(item_slot(row, 1), item_slot(row, 1), ig_s, ig_r, 1, y_dev))
@@ -172,13 +188,12 @@
     start(copy(item_slot(row_x, 0), item_slot(row_x, 0), ig_s, ig_r, 4, y_dev))
     arrived(item_slot(row_y, 1), ig_r, 1)
     start(copy(item_slot(row_y, 1), item_slot(row_y, 1), ig_s, ig_r, 5, x_dev))
-    order = [1] + list(range(n_z - 1, 1, -1)) if n_z > 1 else []
-    for d in order:
-        slot = user_slot(2 * ((z - d + n_z) % n_z) + core)
-        arrived(slot, uz_r, d)
-        start(copy(slot, slot, up_s, up_r, d, p_dev))
-    for d in [0] + order:
-        arrived(user_slot(2 * ((z - d + n_z) % n_z) + 1 - core), up_r, d)
+    for at in near_first:
+        slot = user_slot(2 * at + core)
+        arrived(slot, uz_r, at)
+        start(copy(slot, slot, up_s, up_r, at, p_dev))
+    for at in [z] + near_first:
+        arrived(user_slot(2 * at + 1 - core), up_r, at)
 
     user_sel = u_all[tu]
     user_sel = jnp.where(live, user_sel, 0.0).astype(user_sel.dtype)
@@ -219,14 +234,13 @@
     partner_tu = meta_p[0][0:1, :]
     for h in range(pieces):
         arrived(from_p.at[h], rp_r, h)
-    for d in list(range(1, n_z)) + [0]:
-        at = (z + d) % n_z
+    for at, device in list(zip(others, z_devs)) + [(z, None)]:
         tile, h = at // pieces, at % pieces
-        send_z[d] = jnp.where(my_tu == tile, part_u[2 * h + core], 0.0) + jnp.where(
+        send_z[at] = jnp.where(my_tu == tile, part_u[2 * h + core], 0.0) + jnp.where(
             partner_tu == tile, from_p[h], 0.0
         )
-        if d:
-            start(copy(send_z.at[d], from_z.at[d], rz_s, rz_r, d, z_devs[d]))
+        if device is not None:
+            start(copy(send_z.at[at], from_z.at[z], rz_s, rz_r, z, device, at))
 
     for c in (0, 2, 1, 3):
         second(c)
@@ -237,10 +251,10 @@
         arrived(from_2.at[c], r2_r, c)
         out_i[pl.ds(c * chunk, chunk), :] = (mine + from_2[c]).astype(out_i.dtype)
 
-    total = send_z[0]
-    for d in order:
-        arrived(from_z.at[d], rz_r, d)
-        total = total + from_z[d]
+    total = send_z[z]
+    for at in near_first:
+        arrived(from_z.at[at], rz_r, at)
+        total = total + from_z[at]
     out_u[...] = total.astype(out_u.dtype)
 
     for c in sent:
@@ -265,14 +279,13 @@
     f32, bf16, dma = jnp.float32, jnp.bfloat16, pltpu.SemaphoreType.DMA
     blocks = size // rows_u
     vmem = pl.BlockSpec(memory_space=pltpu.VMEM)
-    smem = pl.BlockSpec(memory_space=pltpu.SMEM)
     anywhere = pl.BlockSpec(memory_space=pl.ANY)
     quarter = (4, rows_i // 4, width)
     pairs = [3, n_z, n_z, 6, blocks // 2, n_z, 4, 4]
     outs = pl.pallas_call(
         functools.partial(kernel, n_z),
         out_shape=(pltpu.VMEM((rows_u, width), bf16), pltpu.VMEM((rows_i, width), bf16)),
-        in_specs=[smem, smem, anywhere, anywhere, anywhere],
+        in_specs=[anywhere] * 5,
         out_specs=(vmem, vmem),
         scratch_shapes=[
             pltpu.VMEM((2 * n_z * rows_u // size, size, width), bf16),
@@ -291,7 +304,9 @@
             pltpu.VMEM(quarter, f32),
             pltpu.VMEM(quarter, f32),
             pltpu.VMEM(quarter, f32),
-            dma((3,)),
+            pltpu.SMEM((2,), jnp.int32),
+            pltpu.SMEM((1, 1), jnp.int32),
+            dma((5,)),
         ]
         + [dma((n,)) for n in pairs for _ in range(2)],
         compiler_params=pltpu.CompilerParams(collective_id=0, has_side_effects=True),

time: 23.3 us -> 22.7 us (0.974)
  Pallas kernels: 21.7 us -> 21 us
    pallas_call x1, Pallas kernels: 21 us -> 20.3 us  [planned(): pl.pallas_call(functools.partial(kernel, n_z), out_shape=(pltpu.VMEM((row...]
where the time goes in v3:
time: 22.7 us; the launch traced here: 22.2 us
  Pallas kernels  21 us (93%)
  between operations  1.29 us (6%)
    pallas_call x1, Pallas kernels, planned(): pl.pallas_call(functools.partial(kernel, n_z), out_shape=(pltpu.VMEM((row...  20.3 us
    pallas_call x1, Pallas kernels, planned(): pl.pallas_call(put, out_shape=[jax.ShapeDtypeStruct(out.shape, out.dtype)...  0.69 us

profile of v3, /device:TPU:0, one launch (start us, length us, event | category | flops | bytes accessed | tf_op | source)
XLA Modules:
  0.0 22.2 jit_solution(7231017160225330356)
XLA Ops:
  1.3 20.3 %shard_map.68 = (bf16[128,128]{1,0:T(8,128)(2,1)S(1)}, bf16[512,128]{1,0:T(8,128)(2,1)S(1)}) custom-call(s32[2]{0:T(128)} %bitcast.3, s32[1,1]{1,0:T(1,128)S(6)} %copy.7.count_in, bf16[128,128]{1,0:T(8,128)(2,1)} %user_in.1, bf16[512,128]{1,0:T(8,128)(2,1)} %item_in.1, bf16[512,512]{1,0:T(8,128)(2,1)} %bitcast.2), custom_call_target="tpu_custom_call" | custom-call | tf_op jit(solution)/shard_map/pallas_call | solution.py:285
  21.6 0.7 %shard_map.69 = (bf16[128,128]{1,0:T(8,128)(2,1)}, bf16[512,128]{1,0:T(8,128)(2,1)}) custom-call(bf16[128,128]{1,0:T(8,128)(2,1)S(1)} %get-tuple-element.4.users, bf16[512,128]{1,0:T(8,128)(2,1)S(1)} %get-tuple-element.5.items), custom_call_target="tpu_custom_call" | custom-call | tf_op jit(solution)/shard_map/pallas_call | solution.py:320

commit v4 on v3

--- a/solution.py
+++ b/solution.py
@@ -65,9 +65,7 @@
     tile_v,
     tile_t,
     meta,
-    meta_x,
-    meta_y,
-    meta_p,
+    metas,
     part_u,
     from_p,
     send_z,
@@ -114,8 +112,8 @@
     z_devs = [(row, 2 * at + core) for at in others]
     near_first = others[::-1]
     rows_u, rows_i = user_in.shape[0], item_in.shape[0]
-    size = tile_v.shape[0]
-    half, chunk = rows_i // 2, rows_i // 4
+    size = tile_v.shape[-1]
+    chunk = rows_i // 4
     pieces = size // rows_u // 2
 
     def user_slot(at):
@@ -123,18 +121,25 @@
         inner = pl.multiple_of(at % blocks * rows_u, rows_u)
         return u_all.at[at // blocks, pl.ds(inner, rows_u)]
 
-    def item_slot(at, part):
-        return i_all.at[at, pl.ds(part * half, half)]
-
-    def copy(src, dst, sends, recvs, at, device, to=None):
+    def item_slot(at, part, parts=2):
+        rows = rows_i // parts
+        return i_all.at[at, pl.ds(part * rows, rows)]
+
+    def copy(src, dst, send, recv, device):
         return pltpu.make_async_remote_copy(
             src_ref=src,
             dst_ref=dst,
-            send_sem=sends.at[at if to is None else to],
-            recv_sem=recvs.at[at],
+            send_sem=send,
+            recv_sem=recv,
             device_id=device,
             device_id_type=MESH,
         )
+
+    def arrived(like, recv):
+        copy(like, like, recv, recv, x_dev).wait_recv()
+
+    def left(like, send):
+        copy(like, like, send, send, x_dev).wait_send()
 
     barrier = pltpu.get_barrier_semaphore()
     peers = [x_dev, y_dev, p_dev] + z_devs
@@ -159,41 +164,40 @@
     my_tu, my_ti, live = meta[0][0:1, :], meta[1][0:1, :], meta[2][0:1, :] > 0
     pl.semaphore_wait(barrier, len(peers))
 
-    sent = []
-
-    def start(c):
-        c.start()
-        sent.append(c)
+    def relay_item(at, part, recv, device):
+        piece = item_slot(at, part, 4)
+        copy(piece, piece, ig_s.at[0], ig_r.at[recv], device).start()
 
     loads[0].wait()
-    for to, device in zip(others, z_devs):
-        start(copy(user_slot(col), user_slot(col), uz_s, uz_r, z, device, to))
-    start(copy(user_slot(col), user_slot(col), up_s, up_r, z, p_dev))
+    own = user_slot(col)
+    for device in z_devs:
+        copy(own, own, uz_s.at[0], uz_r.at[z], device).start()
+    copy(own, own, up_s.at[0], up_r.at[0], p_dev).start()
     loads[1].wait()
-    start(copy(item_slot(row, 0), item_slot(row, 0), ig_s, ig_r, 0, x_dev))
-    start(copy(item_slot(row, 1), item_slot(row, 1), ig_s, ig_r, 1, y_dev))
-    start(copy(item_slot(row, 1), item_slot(row, 1), ig_s, ig_r, 2, x_dev))
-    start(copy(item_slot(row, 0), item_slot(row, 0), ig_s, ig_r, 3, y_dev))
-    start(copy(meta, meta_x, meta_s, meta_r, 0, x_dev))
-    start(copy(meta, meta_y, meta_s, meta_r, 1, y_dev))
-    start(copy(meta, meta_p, meta_s, meta_r, 2, p_dev))
+    for part in range(2):
+        relay_item(row, part, part, x_dev)
+        relay_item(row, 2 + part, 2 + part, y_dev)
+    for part, device in ((1, x_dev), (0, y_dev)):
+        piece = item_slot(row, part)
+        copy(piece, piece, ig_s.at[0], ig_r.at[4], device).start()
+    for at, device in enumerate((x_dev, y_dev, p_dev)):
+        copy(meta, metas.at[at], meta_s.at[0], meta_r.at[0], device).start()
+    meta_x, meta_y, meta_p = metas.at[0], metas.at[1], metas.at[2]
 
     loads[2].wait()
-    tile_t[...] = tile_v[...].T
-
-    def arrived(slot, recvs, at):
-        copy(slot, slot, recvs, recvs, at, x_dev).wait_recv()
-
-    arrived(item_slot(row_x, 0), ig_r, 0)
-    start(copy(item_slot(row_x, 0), item_slot(row_x, 0), ig_s, ig_r, 4, y_dev))
-    arrived(item_slot(row_y, 1), ig_r, 1)
-    start(copy(item_slot(row_y, 1), item_slot(row_y, 1), ig_s, ig_r, 5, x_dev))
+    tile_t[...] = tile_v[...].reshape(size, size).T
+
+    for part in range(2):
+        arrived(item_slot(row_x, part, 4), ig_r.at[part])
+        relay_item(row_x, part, 4, y_dev)
+        arrived(item_slot(row_y, 2 + part, 4), ig_r.at[2 + part])
+        relay_item(row_y, 2 + part, 4, x_dev)
     for at in near_first:
         slot = user_slot(2 * at + core)
-        arrived(slot, uz_r, at)
-        start(copy(slot, slot, up_s, up_r, at, p_dev))
-    for at in [z] + near_first:
-        arrived(user_slot(2 * at + 1 - core), up_r, at)
+        arrived(slot, uz_r.at[at])
+        copy(slot, slot, up_s.at[0], up_r.at[0], p_dev).start()
+    half_users = u_all.at[pl.ds(0, u_all.shape[0] // 2)]
+    arrived(half_users, up_r.at[0])
 
     user_sel = u_all[tu]
     user_sel = jnp.where(live, user_sel, 0.0).astype(user_sel.dtype)
@@ -201,46 +205,44 @@
         tile_t[...], user_sel, preferred_element_type=jnp.float32
     ).reshape(part_i.shape)
     for c in (0, 2, 1, 3):
-        start(copy(part_i.at[c], from_1.at[c], r1_s, r1_r, c, x_dev if c < 2 else y_dev))
-
-    diagonal = 2 * (1 - y) + 1 - x
-    arrived(item_slot(row_x, 1), ig_r, 2)
-    arrived(item_slot(row_y, 0), ig_r, 3)
-    arrived(item_slot(diagonal, 0), ig_r, 4)
-    arrived(item_slot(diagonal, 1), ig_r, 5)
+        copy(
+            part_i.at[c], from_1.at[c], r1_s.at[0], r1_r.at[c], x_dev if c < 2 else y_dev
+        ).start()
+
+    arrived(i_all.at[pl.ds(0, 2)], ig_r.at[4])
     item_sel = i_all[ti]
     item_sel = jnp.where(live, item_sel, 0.0).astype(item_sel.dtype)
-    part_u[...] = jnp.dot(
-        tile_v[...], item_sel, preferred_element_type=jnp.float32
-    ).reshape(part_u.shape)
+
+    def multiply(b):
+        part_u[b] = jnp.dot(tile_v[b], item_sel, preferred_element_type=jnp.float32)
+
     for h in range(pieces):
-        start(copy(part_u.at[2 * h + 1 - core], from_p.at[h], rp_s, rp_r, h, p_dev))
-
-    arrived(meta_x, meta_r, 0)
-    arrived(meta_y, meta_r, 1)
-    arrived(meta_p, meta_r, 2)
+        multiply(2 * h + 1 - core)
+        copy(part_u.at[2 * h + 1 - core], from_p.at[h], rp_s.at[0], rp_r.at[0], p_dev).start()
+    for h in range(pieces):
+        multiply(2 * h + core)
+    arrived(metas, meta_r.at[0])
 
     def second(c):
         other, owner, device = (
             (meta_x, row_y, y_dev) if c < 2 else (meta_y, row_x, x_dev)
         )
         theirs = other[1][0:1, :]
-        arrived(from_1.at[c], r1_r, c)
+        arrived(from_1.at[c], r1_r.at[c])
         send_2[c] = jnp.where(my_ti == owner, part_i[c], 0.0) + jnp.where(
             theirs == owner, from_1[c], 0.0
         )
-        start(copy(send_2.at[c], from_2.at[c], r2_s, r2_r, c, device))
+        copy(send_2.at[c], from_2.at[c], r2_s.at[0], r2_r.at[c], device).start()
 
     partner_tu = meta_p[0][0:1, :]
-    for h in range(pieces):
-        arrived(from_p.at[h], rp_r, h)
+    arrived(from_p, rp_r.at[0])
     for at, device in list(zip(others, z_devs)) + [(z, None)]:
         tile, h = at // pieces, at % pieces
         send_z[at] = jnp.where(my_tu == tile, part_u[2 * h + core], 0.0) + jnp.where(
             partner_tu == tile, from_p[h], 0.0
         )
         if device is not None:
-            start(copy(send_z.at[at], from_z.at[z], rz_s, rz_r, z, device, at))
+            copy(send_z.at[at], from_z.at[z], rz_s.at[0], rz_r.at[0], device).start()
 
     for c in (0, 2, 1, 3):
         second(c)
@@ -248,17 +250,23 @@
     for c in (0, 2, 1, 3):
         theirs = (meta_x if c < 2 else meta_y)[1][0:1, :]
         mine = jnp.where(my_ti == row, part_i[c], 0.0) + jnp.where(theirs == row, from_1[c], 0.0)
-        arrived(from_2.at[c], r2_r, c)
+        arrived(from_2.at[c], r2_r.at[c])
         out_i[pl.ds(c * chunk, chunk), :] = (mine + from_2[c]).astype(out_i.dtype)
 
     total = send_z[z]
+    arrived(from_z.at[pl.ds(0, n_z - 1)], rz_r.at[0])
     for at in near_first:
-        arrived(from_z.at[at], rz_r, at)
         total = total + from_z[at]
     out_u[...] = total.astype(out_u.dtype)
 
-    for c in sent:
-        c.wait_send()
+    left(u_all.at[0, pl.ds(0, (n_z - 1) * rows_u)], uz_s.at[0])
+    left(half_users, up_s.at[0])
+    left(i_all.at[pl.ds(0, 3)], ig_s.at[0])
+    left(metas, meta_s.at[0])
+    left(part_i, r1_s.at[0])
+    left(from_p, rp_s.at[0])
+    left(send_2, r2_s.at[0])
+    left(send_z.at[pl.ds(0, n_z - 1)], rz_s.at[0])
 
 
 def put(users, items, out_u, out_i, sems):
@@ -281,7 +289,7 @@
     vmem = pl.BlockSpec(memory_space=pltpu.VMEM)
     anywhere = pl.BlockSpec(memory_space=pl.ANY)
     quarter = (4, rows_i // 4, width)
-    pairs = [3, n_z, n_z, 6, blocks // 2, n_z, 4, 4]
+    arrivals = [1, n_z, 1, 5, 1, 1, 4, 4]
     outs = pl.pallas_call(
         functools.partial(kernel, n_z),
         out_shape=(pltpu.VMEM((rows_u, width), bf16), pltpu.VMEM((rows_i, width), bf16)),
@@ -290,12 +298,10 @@
         scratch_shapes=[
             pltpu.VMEM((2 * n_z * rows_u // size, size, width), bf16),
             pltpu.VMEM((4, rows_i, width), bf16),
-            pltpu.VMEM((size, size), bf16),
+            pltpu.VMEM((blocks, rows_u, size), bf16),
             pltpu.VMEM((size, size), bf16),
             pltpu.VMEM((3, 8, width), jnp.int32),
-            pltpu.VMEM((3, 8, width), jnp.int32),
-            pltpu.VMEM((3, 8, width), jnp.int32),
-            pltpu.VMEM((3, 8, width), jnp.int32),
+            pltpu.VMEM((3, 3, 8, width), jnp.int32),
             pltpu.VMEM((blocks, rows_u, width), f32),
             pltpu.VMEM((blocks // 2, rows_u, width), f32),
             pltpu.VMEM((n_z, rows_u, width), f32),
@@ -308,14 +314,14 @@
             pltpu.SMEM((1, 1), jnp.int32),
             dma((5,)),
         ]
-        + [dma((n,)) for n in pairs for _ in range(2)],
+        + [dma((n,)) for arrival in arrivals for n in (1, arrival)],
         compiler_params=pltpu.CompilerParams(collective_id=0, has_side_effects=True),
     )(
         tile_coords.reshape(2),
         tile_count,
         user_feats,
         item_feats,
-        tile_values.reshape(size, size),
+        tile_values.reshape(blocks, rows_u, size),
     )
     return pl.pallas_call(
         put,
@@ -338,7 +344,8 @@
             and slots == 1
             and item_feats.shape[0] == size
             and size % (2 * rows_u) == 0
-            and n_col * rows_u % size == 0
+            and n_col * rows_u % (2 * size) == 0
+            and (n_col // 2 - 1) * rows_u <= size
         )
         args = (user_feats, item_feats, tile_values, tile_coords, tile_count)
         return planned(*args, n_z=n_col // 2) if fits else gathered(*args)

time: 22.7 us -> 22.1 us (0.974); the launches traced: 22.2 us -> 22 us
  Pallas kernels: 21 us -> 20.7 us
    pallas_call x1, Pallas kernels: 20.3 us -> 20 us  [planned(): pl.pallas_call(functools.partial(kernel, n_z), out_shape=(pltpu.VMEM((row...]
where the time goes in v4:
time: 22.1 us; the launch traced here: 22 us
  Pallas kernels  20.7 us (94%)
  between operations  1.29 us (6%)
    pallas_call x1, Pallas kernels, planned(): pl.pallas_call(functools.partial(kernel, n_z), out_shape=(pltpu.VMEM((row...  20 us
    pallas_call x1, Pallas kernels, planned(): pl.pallas_call(put, out_shape=[jax.ShapeDtypeStruct(out.shape, out.dtype)...  0.69 us

profile of v4, /device:TPU:0, one launch (start us, length us, event | category | flops | bytes accessed | tf_op | source)
XLA Modules:
  0.0 22.0 jit_solution(12880125123564692326)
XLA Ops:
  1.3 20.0 %shard_map.68 = (bf16[128,128]{1,0:T(8,128)(2,1)S(1)}, bf16[512,128]{1,0:T(8,128)(2,1)S(1)}) custom-call(s32[2]{0:T(128)} %bitcast.3, s32[1,1]{1,0:T(1,128)S(6)} %copy.7.count_in, bf16[128,128]{1,0:T(8,128)(2,1)} %user_in.1, bf16[512,128]{1,0:T(8,128)(2,1)} %item_in.1, bf16[4,128,512]{2,1,0:T(8,128)(2,1)} %bitcast.2), custom_call_target="tpu_custom_call" | custom-call | tf_op jit(solution)/shard_map/pallas_call | solution.py:293
  21.3 0.7 %shard_map.69 = (bf16[128,128]{1,0:T(8,128)(2,1)}, bf16[512,128]{1,0:T(8,128)(2,1)}) custom-call(bf16[128,128]{1,0:T(8,128)(2,1)S(1)} %get-tuple-element.4.users, bf16[512,128]{1,0:T(8,128)(2,1)S(1)} %get-tuple-element.5.items), custom_call_target="tpu_custom_call" | custom-call | tf_op jit(solution)/shard_map/pallas_call | solution.py:326

commit v5 on v4

--- a/solution.py
+++ b/solution.py
@@ -70,6 +70,7 @@
     from_p,
     send_z,
     from_z,
+    via,
     part_i,
     from_1,
     send_2,
@@ -77,6 +78,7 @@
     coords,
     count,
     load_sem,
+    via_r,
     meta_s,
     meta_r,
     uz_s,
@@ -111,6 +113,9 @@
     others = [far_first(at) for at in range(n_z - 1)]
     z_devs = [(row, 2 * at + core) for at in others]
     near_first = others[::-1]
+    flip = z // 2
+    far, cross, beside = 3 - 3 * flip, 2 - flip, z + 1 - 2 * (z % 2)
+    edge = z % 3 == 0
     rows_u, rows_i = user_in.shape[0], item_in.shape[0]
     size = tile_v.shape[-1]
     chunk = rows_i // 4
@@ -213,14 +218,16 @@
     item_sel = i_all[ti]
     item_sel = jnp.where(live, item_sel, 0.0).astype(item_sel.dtype)
 
-    def multiply(b):
-        part_u[b] = jnp.dot(tile_v[b], item_sel, preferred_element_type=jnp.float32)
-
+    def multiply(owner):
+        rows = jnp.concatenate([tile_v[2 * h + owner] for h in range(pieces)], axis=0)
+        product = jnp.dot(rows, item_sel, preferred_element_type=jnp.float32)
+        for h in range(pieces):
+            part_u[2 * h + owner] = product[h * rows_u : (h + 1) * rows_u]
+
+    multiply(1 - core)
     for h in range(pieces):
-        multiply(2 * h + 1 - core)
         copy(part_u.at[2 * h + 1 - core], from_p.at[h], rp_s.at[0], rp_r.at[0], p_dev).start()
-    for h in range(pieces):
-        multiply(2 * h + core)
+    multiply(core)
     arrived(metas, meta_r.at[0])
 
     def second(c):
@@ -236,16 +243,36 @@
 
     partner_tu = meta_p[0][0:1, :]
     arrived(from_p, rp_r.at[0])
-    for at, device in list(zip(others, z_devs)) + [(z, None)]:
+
+    def combine(at):
         tile, h = at // pieces, at % pieces
         send_z[at] = jnp.where(my_tu == tile, part_u[2 * h + core], 0.0) + jnp.where(
             partner_tu == tile, from_p[h], 0.0
         )
-        if device is not None:
-            copy(send_z.at[at], from_z.at[z], rz_s.at[0], rz_r.at[0], device).start()
+
+    def along_z(at, dst, recv, to):
+        device = (row, 2 * to + core)
+        copy(send_z.at[at], dst, rz_s.at[0], recv, device).start()
+
+    combine(cross)
+
+    @pl.when(edge)
+    def _():
+        along_z(cross, via, via_r.at[0], beside)
+
+    for at in (far, beside):
+        combine(at)
+        along_z(at, from_z.at[z], rz_r.at[0], at)
+    combine(z)
 
     for c in (0, 2, 1, 3):
         second(c)
+
+    @pl.when(jnp.logical_not(edge))
+    def _():
+        arrived(via, via_r.at[0])
+        send_z[cross] = send_z[cross] + via[...]
+        along_z(cross, from_z.at[z], rz_r.at[0], cross)
 
     for c in (0, 2, 1, 3):
         theirs = (meta_x if c < 2 else meta_y)[1][0:1, :]
@@ -253,11 +280,20 @@
         arrived(from_2.at[c], r2_r.at[c])
         out_i[pl.ds(c * chunk, chunk), :] = (mine + from_2[c]).astype(out_i.dtype)
 
-    total = send_z[z]
-    arrived(from_z.at[pl.ds(0, n_z - 1)], rz_r.at[0])
-    for at in near_first:
-        total = total + from_z[at]
-    out_u[...] = total.astype(out_u.dtype)
+    def finish(sources):
+        arrived(from_z.at[pl.ds(0, len(sources))], rz_r.at[0])
+        total = send_z[z]
+        for at in sources:
+            total = total + from_z[at]
+        out_u[...] = total.astype(out_u.dtype)
+
+    @pl.when(edge)
+    def _():
+        finish([beside, cross, far])
+
+    @pl.when(jnp.logical_not(edge))
+    def _():
+        finish([beside, cross])
 
     left(u_all.at[0, pl.ds(0, (n_z - 1) * rows_u)], uz_s.at[0])
     left(half_users, up_s.at[0])
@@ -306,6 +342,7 @@
             pltpu.VMEM((blocks // 2, rows_u, width), f32),
             pltpu.VMEM((n_z, rows_u, width), f32),
             pltpu.VMEM((n_z, rows_u, width), f32),
+            pltpu.VMEM((rows_u, width), f32),
             pltpu.VMEM(quarter, f32),
             pltpu.VMEM(quarter, f32),
             pltpu.VMEM(quarter, f32),
@@ -313,6 +350,7 @@
             pltpu.SMEM((2,), jnp.int32),
             pltpu.SMEM((1, 1), jnp.int32),
             dma((5,)),
+            dma((1,)),
         ]
         + [dma((n,)) for arrival in arrivals for n in (1, arrival)],
         compiler_params=pltpu.CompilerParams(collective_id=0, has_side_effects=True),
@@ -340,7 +378,7 @@
         rows_u = user_feats.shape[0]
         fits = (
             n_row == 4
-            and n_col % 2 == 0
+            and n_col == 8
             and slots == 1
             and item_feats.shape[0] == size
             and size % (2 * rows_u) == 0

time: 22.1 us -> 22.3 us (level)
  no operation moved by 1% of the time
where the time goes in v5:
time: 22.3 us; the launch traced here: 22.2 us
  Pallas kernels  20.9 us (94%)
  between operations  1.29 us (6%)
    pallas_call x1, Pallas kernels, planned(): pl.pallas_call(functools.partial(kernel, n_z), out_shape=(pltpu.VMEM((row...  20.2 us
    pallas_call x1, Pallas kernels, planned(): pl.pallas_call(put, out_shape=[jax.ShapeDtypeStruct(out.shape, out.dtype)...  0.69 us

profile of v5, /device:TPU:0, one launch (start us, length us, event | category | flops | bytes accessed | tf_op | source)
XLA Modules:
  0.0 22.2 jit_solution(7295502138195091096)
XLA Ops:
  1.3 20.2 %shard_map.68 = (bf16[128,128]{1,0:T(8,128)(2,1)S(1)}, bf16[512,128]{1,0:T(8,128)(2,1)S(1)}) custom-call(s32[2]{0:T(128)} %bitcast.3, s32[1,1]{1,0:T(1,128)S(6)} %copy.7.count_in, bf16[128,128]{1,0:T(8,128)(2,1)} %user_in.1, bf16[512,128]{1,0:T(8,128)(2,1)} %item_in.1, bf16[4,128,512]{2,1,0:T(8,128)(2,1)} %bitcast.2), custom_call_target="tpu_custom_call" | custom-call | tf_op jit(solution)/shard_map/pallas_call | solution.py:329
  21.5 0.7 %shard_map.69 = (bf16[128,128]{1,0:T(8,128)(2,1)}, bf16[512,128]{1,0:T(8,128)(2,1)}) custom-call(bf16[128,128]{1,0:T(8,128)(2,1)S(1)} %get-tuple-element.4.users, bf16[512,128]{1,0:T(8,128)(2,1)S(1)} %get-tuple-element.5.items), custom_call_target="tpu_custom_call" | custom-call | tf_op jit(solution)/shard_map/pallas_call | solution.py:364

commit v6 on v4

--- a/solution.py
+++ b/solution.py
@@ -213,14 +213,16 @@
     item_sel = i_all[ti]
     item_sel = jnp.where(live, item_sel, 0.0).astype(item_sel.dtype)
 
-    def multiply(b):
-        part_u[b] = jnp.dot(tile_v[b], item_sel, preferred_element_type=jnp.float32)
-
+    def multiply(owner):
+        rows = jnp.concatenate([tile_v[2 * h + owner] for h in range(pieces)], axis=0)
+        product = jnp.dot(rows, item_sel, preferred_element_type=jnp.float32)
+        for h in range(pieces):
+            part_u[2 * h + owner] = product[h * rows_u : (h + 1) * rows_u]
+
+    multiply(1 - core)
     for h in range(pieces):
-        multiply(2 * h + 1 - core)
         copy(part_u.at[2 * h + 1 - core], from_p.at[h], rp_s.at[0], rp_r.at[0], p_dev).start()
-    for h in range(pieces):
-        multiply(2 * h + core)
+    multiply(core)
     arrived(metas, meta_r.at[0])
 
     def second(c):

time: 22.1 us -> 22 us (level)
  no operation moved by 1% of the time
where the time goes in v6:
time: 22 us; the launch traced here: 21.8 us
  Pallas kernels  20.5 us (93%)
  between operations  1.29 us (6%)
    pallas_call x1, Pallas kernels, planned(): pl.pallas_call(functools.partial(kernel, n_z), out_shape=(pltpu.VMEM((row...  19.8 us
    pallas_call x1, Pallas kernels, planned(): pl.pallas_call(put, out_shape=[jax.ShapeDtypeStruct(out.shape, out.dtype)...  0.69 us

profile of v6, /device:TPU:0, one launch (start us, length us, event | category | flops | bytes accessed | tf_op | source)
XLA Modules:
  0.0 21.8 jit_solution(5649653339247110656)
XLA Ops:
  1.3 19.8 %shard_map.68 = (bf16[128,128]{1,0:T(8,128)(2,1)S(1)}, bf16[512,128]{1,0:T(8,128)(2,1)S(1)}) custom-call(s32[2]{0:T(128)} %bitcast.3, s32[1,1]{1,0:T(1,128)S(6)} %copy.7.count_in, bf16[128,128]{1,0:T(8,128)(2,1)} %user_in.1, bf16[512,128]{1,0:T(8,128)(2,1)} %item_in.1, bf16[4,128,512]{2,1,0:T(8,128)(2,1)} %bitcast.2), custom_call_target="tpu_custom_call" | custom-call | tf_op jit(solution)/shard_map/pallas_call | solution.py:295
  21.1 0.7 %shard_map.69 = (bf16[128,128]{1,0:T(8,128)(2,1)}, bf16[512,128]{1,0:T(8,128)(2,1)}) custom-call(bf16[128,128]{1,0:T(8,128)(2,1)S(1)} %get-tuple-element.4.users, bf16[512,128]{1,0:T(8,128)(2,1)S(1)} %get-tuple-element.5.items), custom_call_target="tpu_custom_call" | custom-call | tf_op jit(solution)/shard_map/pallas_call | solution.py:328
